TPU v7x, 32 devices: a whole 2x2x4 slice. The times are simulated.
32 devices in a mesh: patch: 2 (over y), gz: 4 (over z), row: 4 (over x, core).
Axes of the slice: x: 2, y: 2, z: 4, core: 2. Of those that a mesh axis runs over, the one named last changes fastest.
Arguments:
- contrast: bfloat16 [32, 128, 1024], P(('patch', 'gz'), 'row'), parts along dimension 0, may hold values from -6 to 6
- lens_weight: float32 [16], P('gz'), may hold values from 0.05 to 0.5
- distances: float32 [2, 16], P(None, 'gz'), may hold values from 1.25 to 25, as said below
Outputs:
- convergence: float32 [32, 128, 1024], P(('patch', 'gz'), 'row'), parts along dimension 0
There are 2 independent parts, one for each index of `patch`. A program takes and returns all parts, laid end to end along the dimension named above; an argument that names none is the same for every part. Nothing has to cross between parts.
Inputs may be any that keep to these rules, and one draw needn't show every extreme that they name: `distances`: both rows rise along the slices, and each slice's lens distance lies below its source distance, which lies below the next slice's lens distance.
All inputs are finite; a program needn't handle non-finite values.
Results may differ from a plain program's by a relative error of at most 0.0049.
Values may be sent and summed in bfloat16 or wider, within the bound.
A program may use at most 64 MiB of HBM per device.

v0:
```python
import math

import jax
import jax.numpy as jnp
from jax import lax
from jax.sharding import PartitionSpec as P

SMOOTH_TAPS = (0.0625, 0.1875, 0.5, 0.1875, 0.0625)


def with_halo(block, sides, width):
    for axis, dim in sides:
        count = lax.axis_size(axis)
        forward = [(i, i + 1) for i in range(count - 1)]
        backward = [(target, source) for source, target in forward]
        low = lax.ppermute(
            lax.slice_in_dim(block, block.shape[dim] - width, None, axis=dim), axis, forward
        )
        high = lax.ppermute(lax.slice_in_dim(block, 0, width, axis=dim), axis, backward)
        block = jnp.concatenate([low, block, high], axis=dim)
    return block


def entering(x, axis, combine, identity):
    length, here = (lax.axis_size(axis), lax.axis_index(axis))
    everything = lax.all_gather(x, axis)
    start = jnp.broadcast_to(jnp.asarray(identity, x.dtype), x.shape)

    def step(k, before):
        reached = k < here
        new = combine(before, everything[k])
        return jnp.where(reached, new, before)

    return lax.fori_loop(0, length, step, start)


def beam_table(count):
    index = jnp.arange(count).astype(jnp.float32)
    offset = index[:, None] - index[None, :]
    return (jnp.exp(-offset * offset) / math.sqrt(math.pi)).astype(jnp.bfloat16)


def smooth_rows(padded, count):
    total = SMOOTH_TAPS[0] * padded[..., 0:count, :]
    for offset in range(1, 5):
        total = total + SMOOTH_TAPS[offset] * padded[..., offset : offset + count, :]
    return total


def apply_beam(slabs, beam):
    flat = slabs.reshape(-1, slabs.shape[-1])
    across = jnp.dot(flat, beam, preferred_element_type=jnp.float32)
    return across.reshape(slabs.shape)


def add_pairs(earlier, later):
    return earlier + later


def local(contrast, lens_weight, distances):
    slices_dev = contrast.shape[0]
    rows_dev = contrast.shape[1]
    near = distances[0]
    far = distances[1]
    beam = beam_table(contrast.shape[2])
    padded = with_halo(contrast, (("row", 1),), 2)
    fields = smooth_rows(apply_beam(padded, beam), rows_dev)
    run_plain = jnp.zeros(fields.shape[1:], jnp.float32)
    run_dist = jnp.zeros(fields.shape[1:], jnp.float32)
    plain_list = []
    dist_list = []
    for within in range(slices_dev):
        run_plain = run_plain + lens_weight[within] * fields[within]
        run_dist = run_dist + lens_weight[within] * near[within] * fields[within]
        plain_list.append(run_plain)
        dist_list.append(run_dist)
    totals = jnp.stack([run_plain, run_dist])
    before = entering(totals, "gz", add_pairs, jnp.zeros_like(totals))
    maps = []
    for within in range(slices_dev):
        plain_here = before[0] + plain_list[within]
        dist_here = before[1] + dist_list[within]
        maps.append(plain_here - dist_here / far[within])
    result = jnp.stack(maps)
    return result


def solution(mesh):
    return jax.shard_map(
        local,
        mesh=mesh,
        in_specs=(P(("patch", "gz"), "row", None), P("gz"), P(None, "gz")),
        out_specs=P(("patch", "gz"), "row", None),
        check_vma=False,
    )
```

profile of v0, /device:TPU:0, one launch (start us, length us, event | category | flops | bytes accessed | tf_op | source)
XLA Modules:
  0.0 73.9 jit_solution(9007386232729949405)
XLA Ops:
  6.5 0.0 all-gather.3.cloned.1.call-start
  6.5 0.9 %fusion.19 = (bf16[4,2,1024]{2,1,0:T(2,128)(2,1)S(1)}, bf16[4,2,1024]{2,1,0:T(2,128)(2,1)S(1)}) fusion(bf16[4,32,1024]{2,1,0:T(8,128)(2,1)} %param.5), kind=kLoop, calls=%fused_computation.40 | loop fusion | bytes 65536 | tf_op jit(solution)/shard_map/slice | solution.py:17
  7.4 2.4 %collective-permute-start = (bf16[4,2,1024]{2,1,0:T(2,128)(2,1)S(1)}, bf16[4,2,1024]{2,1,0:T(2,128)(2,1)S(1)}, u32[]{:S(2)}, u32[]{:S(2)}) collective-permute-start(bf16[4,2,1024]{2,1,0:T(2,128)(2,1)S(1)} %get-tuple-element.117), channel_id=1, source_target_pairs={{0,1},{1,2},{2,3},{4,5},{5,6},{6,7},{8,9},{9,10},{10,11},{12,13},{... | collective-permute-start | bytes 49160 | tf_op jit(solution)/shard_map/ppermute | solution.py:16
  9.8 1.3 %collective-permute-start.1 = (bf16[4,2,1024]{2,1,0:T(2,128)(2,1)S(1)}, bf16[4,2,1024]{2,1,0:T(2,128)(2,1)S(1)}, u32[]{:S(2)}, u32[]{:S(2)}) collective-permute-start(bf16[4,2,1024]{2,1,0:T(2,128)(2,1)S(1)} %get-tuple-element.118), channel_id=1, source_target_pairs={{1,0},{2,1},{3,2},{5,4},{6,5},{7,6},{9,8},{10,9},{11,10},{13,12},{... | collective-permute-start | bytes 49160 | tf_op jit(solution)/shard_map/ppermute | solution.py:19
  11.1 1.6 %fusion.20 = (f32[1,1]{1,0:T(1,128)}, f32[1,1]{1,0:T(1,128)}, f32[1,1]{1,0:T(1,128)}, f32[1,1]{1,0:T(1,128)}, f32[1,1]{1,0:T(1,128)}, /*index=5*/f32[1,1]{1,0:T(1,128)}, f32[1,1]{1,0:T(1,128)}, f32[1,1]{1,0:T(1,128)}) fusion(f32[2,4]{1,0:T(2,128)} %param.7), kind=kLoop, calls=%fused_computation.41 | loop fusion | bytes 64 | tf_op jit(solution)/shard_map/slice | solution.py:83
  12.8 1.4 %fusion.21 = (f32[1]{0:T(128)}, f32[1]{0:T(128)}, f32[1]{0:T(128)}, f32[1]{0:T(128)}) fusion(f32[4]{0:T(128)} %param.6), kind=kLoop, calls=%fused_computation.42 | loop fusion | bytes 32 | tf_op jit(solution)/shard_map/slice | solution.py:73
  19.3 0.0 collective-permute-done
  19.3 0.0 collective-permute-done.1
  19.3 2.3 %fusion.4 = f32[4,36,1024]{2,1,0:T(8,128)S(1)} fusion(f32[1024]{0:T(1024)S(1)} %iota_convert_fusion, bf16[4,2,1024]{2,1,0:T(2,128)(2,1)S(1)} %collective-permute-done.1, bf16[4,32,1024]{2,1,0:T(8,128)(2,1)} %param.5, bf16[4,2,1024]{2,1,0:T(2,128)(2,1)S(1)} %collective-permute-done), kind=kOutput, calls=%fused_computation.6 | convolution fusion | flops 308117504 | bytes 888832 | tf_op jit(solution)/shard_map/dot_general | solution.py:52
  21.6 0.3 fusion.8
  21.9 2.7 %multiply_add_fusion.3 = (f32[1,32,1024]{2,1,0:T(8,128)S(1)}, f32[1,32,1024]{2,1,0:T(8,128)S(1)}, f32[1,32,1024]{2,1,0:T(8,128)S(1)}, f32[1,32,1024]{2,1,0:T(8,128)S(1)}) fusion(f32[4,32,1024]{2,1,0:T(8,128)S(1)} %fusion.8, f32[]{:T(128)} %bitcast.4, f32[]{:T(128)} %bitcast.3, f32[]{:T(128)} %bitcast.2, f32[]{:T(128)} %bitcast, f32[]{:T(128)S(6)} %mul.133, ...), kind=kLoop, calls=%fused_computation.32 | loop fusion | flops 458752 | bytes 1048608 | tf_op jit(solution)/shard_map/add | solution.py:73
  24.6 0.7 pad_maximum_fusion.1
  25.3 0.0 all-gather.3.cloned.1.call-update
  25.3 32.7 %all-gather.3.cloned.1.call-done = f32[8,32,1024]{2,1,0:T(8,128)} async-done(((f32[2,32,1024]{2,1,0:T(8,128)}), f32[8,32,1024]{2,1,0:T(8,128)}) %all-gather.3.cloned.1.call-update) | async-done | bytes 1048592 | tf_op jit(solution)/shard_map/all_gather | solution.py:26
  58.1 4.3 %while.14 = (s32[]{:T(128)}, f32[2,32,1024]{2,1,0:T(8,128)S(1)}, s32[]{:T(128)}, f32[4,2,32,1024]{3,2,1,0:T(8,128)}, s32[]{:T(128)}, /*index=5*/s32[]{:T(128)}) while((s32[]{:T(128)}, f32[2,32,1024]{2,1,0:T(8,128)S(1)}, s32[]{:T(128)}, f32[4,2,32,1024]{3,2,1,0:T(8,128)}, s32[]{:T(128)}, /*index=5*/s32[]{:T(128)}) %tuple.54), condition=%wide.region_1.2_spmd.clone, body=%wide.region_0.1_spmd.clone.sunk | while | flops 196612 | bytes 786525 | solution.py:34
  58.1 1.0 %add_select_fusion.2 = f32[2,32,1024]{2,1,0:T(8,128)S(1)} fusion(f32[2,32,1024]{2,1,0:T(8,128)S(1)} %get-tuple-element.163, f32[4,2,32,1024]{3,2,1,0:T(8,128)} %get-tuple-element.171, s32[]{:T(128)} %get-tuple-element.162, pred[]{:T(512)S(6)} %compare.3, pred[]{:T(512)S(6)} %lt.21), kind=kLoop, calls=%fused_computation.clone.1 | loop fusion | flops 196608 | bytes 786438 | tf_op jit(solution)/shard_map/while/body/eval_jaxpr/jit(_where)/select_n | solution.py:32
  59.1 1.0 %add_select_fusion.2 = f32[2,32,1024]{2,1,0:T(8,128)S(1)} fusion(f32[2,32,1024]{2,1,0:T(8,128)S(1)} %get-tuple-element.163, f32[4,2,32,1024]{3,2,1,0:T(8,128)} %get-tuple-element.171, s32[]{:T(128)} %get-tuple-element.162, pred[]{:T(512)S(6)} %compare.3, pred[]{:T(512)S(6)} %lt.21), kind=kLoop, calls=%fused_computation.clone.1 | loop fusion | flops 196608 | bytes 786438 | tf_op jit(solution)/shard_map/while/body/eval_jaxpr/jit(_where)/select_n | solution.py:32
  60.2 1.0 %add_select_fusion.2 = f32[2,32,1024]{2,1,0:T(8,128)S(1)} fusion(f32[2,32,1024]{2,1,0:T(8,128)S(1)} %get-tuple-element.163, f32[4,2,32,1024]{3,2,1,0:T(8,128)} %get-tuple-element.171, s32[]{:T(128)} %get-tuple-element.162, pred[]{:T(512)S(6)} %compare.3, pred[]{:T(512)S(6)} %lt.21), kind=kLoop, calls=%fused_computation.clone.1 | loop fusion | flops 196608 | bytes 786438 | tf_op jit(solution)/shard_map/while/body/eval_jaxpr/jit(_where)/select_n | solution.py:32
  61.3 1.0 %add_select_fusion.2 = f32[2,32,1024]{2,1,0:T(8,128)S(1)} fusion(f32[2,32,1024]{2,1,0:T(8,128)S(1)} %get-tuple-element.163, f32[4,2,32,1024]{3,2,1,0:T(8,128)} %get-tuple-element.171, s32[]{:T(128)} %get-tuple-element.162, pred[]{:T(512)S(6)} %compare.3, pred[]{:T(512)S(6)} %lt.21), kind=kLoop, calls=%fused_computation.clone.1 | loop fusion | flops 196608 | bytes 786438 | tf_op jit(solution)/shard_map/while/body/eval_jaxpr/jit(_where)/select_n | solution.py:32
  62.3 0.7 divide_subtract_fusion
  63.0 3.2 %divide_subtract_fusion.3 = (f32[1,32,1024]{2,1,0:T(8,128)S(1)}, f32[1,32,1024]{2,1,0:T(8,128)S(1)}, f32[1,32,1024]{2,1,0:T(8,128)S(1)}) fusion(f32[4,32,1024]{2,1,0:T(8,128)S(1)} %fusion.8, f32[2,32,1024]{2,1,0:T(8,128)S(1)} %get-tuple-element.84, f32[]{:T(128)} %bitcast.10, f32[]{:T(128)S(6)} %mul.124, f32[]{:T(128)} %bitcast, f32[]{:T(128)} %bitcast.12, ...), kind=kLoop, calls=%fused_computation.28 | loop fusion | flops 589824 | bytes 1179676 | tf_op jit(solution)/shard_map/sub | solution.py:83
  66.2 0.8 %pad_maximum_fusion = f32[4,32,1024]{2,1,0:T(8,128)} fusion(f32[1,32,1024]{2,1,0:T(8,128)S(1)} %divide_subtract_fusion, f32[1,32,1024]{2,1,0:T(8,128)S(1)} %get-tuple-element.113, f32[1,32,1024]{2,1,0:T(8,128)S(1)} %get-tuple-element.114, f32[1,32,1024]{2,1,0:T(8,128)S(1)} %get-tuple-element.112), kind=kLoop, calls=%fused_computation.18 | loop fusion | flops 393216 | bytes 1048576 | tf_op jit(solution)/shard_map/stack | solution.py:84
  (2 shorter events, 0.0 us)
Async XLA Ops:
  6.5 51.5 %all-gather.3.cloned.1.call-start = ((), (), s32[]{:S(2)}) async-start(), calls=%async_computation | async-start | bytes 1310720 | tf_op jit(solution)/shard_map/all_gather | solution.py:26
  7.4 11.8 %collective-permute-start = (bf16[4,2,1024]{2,1,0:T(2,128)(2,1)S(1)}, bf16[4,2,1024]{2,1,0:T(2,128)(2,1)S(1)}, u32[]{:S(2)}, u32[]{:S(2)}) collective-permute-start(bf16[4,2,1024]{2,1,0:T(2,128)(2,1)S(1)} %get-tuple-element.117), channel_id=1, source_target_pairs={{0,1},{1,2},{2,3},{4,5},{5,6},{6,7},{8,9},{9,10},{10,11},{12,13},{... | collective-permute-start | bytes 49160 | tf_op jit(solution)/shard_map/ppermute | solution.py:16
  9.8 9.4 %collective-permute-start.1 = (bf16[4,2,1024]{2,1,0:T(2,128)(2,1)S(1)}, bf16[4,2,1024]{2,1,0:T(2,128)(2,1)S(1)}, u32[]{:S(2)}, u32[]{:S(2)}) collective-permute-start(bf16[4,2,1024]{2,1,0:T(2,128)(2,1)S(1)} %get-tuple-element.118), channel_id=1, source_target_pairs={{1,0},{2,1},{3,2},{5,4},{6,5},{7,6},{9,8},{10,9},{11,10},{13,12},{... | collective-permute-start | bytes 49160 | tf_op jit(solution)/shard_map/ppermute | solution.py:19
Sparse Core Ops, SparseCore 0:
  25.4 32.5 all-gather.2
where the time goes:
time: 74.5 us; the launch traced here: 73.9 us
  waiting for transfers between devices  32.7 us (44%)
  between operations  18.5 us (25%)
  other arithmetic  12.6 us (17%)
  local copies, waits for them, and re-layouts  3.98 us (5%)
  starting transfers between devices  3.69 us (5%)
  matrix products  2.3 us (3%)
    all_gather x1, waiting for transfers between devices, entering(): everything = lax.all_gather(x, axis)  32.7 us
    select_n x4, other arithmetic, step(): return jnp.where(reached, new, before)  4.18 us
    sub x2, other arithmetic, local(): maps.append(plain_here - dist_here / far[within])  3.88 us
    add x1, other arithmetic, local(): run_plain = run_plain + lens_weight[within] * fields[within]  2.66 us
    ppermute x1, starting transfers between devices, with_halo(): lax.ppermute(lax.slice_in_dim(block, block.shape[dim] - width, None, axis...  2.4 us
    dot_general x1, matrix products, apply_beam(): across = jnp.dot(flat, beam, preferred_element_type=jnp.float32)  2.3 us
    slice x1, local copies, waits for them, and re-layouts, local(): maps.append(plain_here - dist_here / far[within])  1.65 us
  transfers between devices with their start and end apart: 3, of which 1 were waited for; matrix products, arithmetic and copies ran while one was open for 4% of the time, Pallas kernels for 0%

commit v1 on v0

v1 whole, which is shorter than its diff:
```python
import functools
import math

import jax
import jax.numpy as jnp
from jax import lax
from jax.experimental import pallas as pl
from jax.experimental.pallas import tpu as pltpu
from jax.sharding import PartitionSpec as P

MESH = pl.DeviceIdType.MESH
BLOCK = 256
REACH = 128
EDGE = 8
TAPS = (0.5, 0.1875, 0.0625)


def filter_rows(x):
    count = x.shape[0]
    near = pltpu.roll(x, 1, 0) + pltpu.roll(x, count - 1, 0)
    far = pltpu.roll(x, 2, 0) + pltpu.roll(x, count - 2, 0)
    return TAPS[0] * x + TAPS[1] * near + TAPS[2] * far


def kernel(
    n_gz, n_row, c_hbm, weight_ref, dist_ref, out_ref,
    c_ref, beam_ref, acc_ref, halo_out, halo_in, dist_out, dist_in, plain_ref,
    sent, got, load_sem, halo_send, halo_recv, dist_sems, chain_send, chain_recv,
):
    slices, rows, cols = c_ref.shape
    blocks = cols // BLOCK
    chunks = 2 * blocks
    gz = lax.axis_index("gz")
    row = lax.axis_index("row")
    has_up, has_down = row > 0, row < n_row - 1
    has_prev, has_next = gz > 0, gz < n_gz - 1
    up, down = {"row": row - 1}, {"row": row + 1}
    prev, nxt = {"gz": gz - 1}, {"gz": gz + 1}

    load = pltpu.make_async_copy(c_hbm, c_ref, load_sem)
    load.start()
    barrier = pltpu.get_barrier_semaphore()
    for there, device in ((has_up, up), (has_down, down), (has_prev, prev)):
        @pl.when(there)
        def _(device=device):
            pl.semaphore_signal(barrier, inc=1, device_id=device, device_id_type=MESH)

    def halo_copy(side, device):
        return pltpu.make_async_remote_copy(
            src_ref=halo_out.at[side], dst_ref=halo_in.at[1 - side],
            send_sem=halo_send.at[side], recv_sem=halo_recv.at[1 - side],
            device_id=device, device_id_type=MESH,
        )

    def chain_copy(chunk):
        return pltpu.make_async_remote_copy(
            src_ref=sent.at[chunk], dst_ref=got.at[chunk],
            send_sem=chain_send.at[chunk], recv_sem=chain_recv.at[chunk],
            device_id=nxt, device_id_type=MESH,
        )

    dist_copy = pltpu.make_async_remote_copy(
        src_ref=dist_out, dst_ref=dist_in, send_sem=dist_sems.at[0],
        recv_sem=dist_sems.at[1], device_id=nxt, device_id_type=MESH,
    )

    dist_out[...] = jnp.full(dist_out.shape, dist_ref[1, slices - 1], jnp.float32)
    window = BLOCK + 2 * REACH
    source = lax.broadcasted_iota(jnp.int32, (window, BLOCK), 0)
    target = lax.broadcasted_iota(jnp.int32, (window, BLOCK), 1)
    offset = (source - REACH - target).astype(jnp.float32)
    beam_ref[...] = (jnp.exp(-offset * offset) / math.sqrt(math.pi)).astype(jnp.bfloat16)
    ones = jnp.ones((1, BLOCK), jnp.float32)
    weight = [ones * weight_ref[i] for i in range(slices)]
    weight_near = [weight[i] * dist_ref[0, i] for i in range(slices)]
    far = [ones * dist_ref[1, i] for i in range(slices)]
    inverse = [1.0 / far[i] for i in range(slices)]

    load.wait()
    place = lax.broadcasted_iota(jnp.int32, (2 * slices, cols), 0) // 2
    for side, start in ((0, 0), (1, rows - 2)):
        base = 0 if side == 0 else rows - 16
        packed = jnp.zeros((2 * slices, cols), jnp.float32)
        for i in range(slices):
            piece = c_ref[i, base : base + 16, :].astype(jnp.float32)
            piece = piece[0:8] if side == 0 else piece[8:16]
            piece = pltpu.roll(piece, (2 * i + (0 if side == 0 else 2)) % 8, 0)
            packed = jnp.where(place == i, piece, packed)
        halo_out[side] = packed.astype(halo_out.dtype)

    @pl.when(jnp.logical_not(has_up))
    def _():
        halo_in[0] = jnp.zeros(halo_in.shape[1:], halo_in.dtype)

    @pl.when(jnp.logical_not(has_down))
    def _():
        halo_in[1] = jnp.zeros(halo_in.shape[1:], halo_in.dtype)

    peers = sum(there.astype(jnp.int32) for there in (has_up, has_down, has_next))
    pl.semaphore_wait(barrier, peers)

    for there, side, device in ((has_up, 0, up), (has_down, 1, down)):
        @pl.when(there)
        def _(side=side, device=device):
            halo_copy(side, device).start()

    @pl.when(has_next)
    def _():
        dist_copy.start()

    def across(x, low, high, shift):
        return jnp.dot(
            x, beam_ref[low - shift : high - shift, :], preferred_element_type=jnp.float32
        )

    def span(block):
        shift = block * BLOCK - REACH
        return max(shift, 0), min(shift + window, cols), shift

    def advance(chunk, columns, parts):
        plain = jnp.zeros(parts[0].shape, jnp.float32)
        dist = jnp.zeros(parts[0].shape, jnp.float32)
        maps = []
        for i in range(slices):
            plain = plain + weight[i] * parts[i]
            dist = dist + weight_near[i] * parts[i]
            maps.append(plain - dist * inverse[i])
        put(chunk, columns, maps)
        plain_ref[chunk] = plain

        @pl.when(jnp.logical_and(has_next, jnp.logical_not(has_prev)))
        def _():
            sent[chunk, 0] = plain.astype(sent.dtype)
            sent[chunk, 1] = maps[-1].astype(sent.dtype)
            chain_copy(chunk).start()

    def put(chunk, columns, maps):
        for i in range(slices):
            if chunk < blocks:
                out_ref[i, EDGE : rows - EDGE, columns] = maps[i]
            else:
                out_ref[i, 0:EDGE, columns] = maps[i][0:EDGE]
                out_ref[i, rows - EDGE : rows, columns] = maps[i][EDGE:]

    def take(chunk, columns, i):
        if chunk < blocks:
            return out_ref[i, EDGE : rows - EDGE, columns]
        return jnp.concatenate(
            [out_ref[i, 0:EDGE, columns], out_ref[i, rows - EDGE : rows, columns]], axis=0
        )

    for block in range(blocks):
        columns = slice(block * BLOCK, (block + 1) * BLOCK)
        low, high, shift = span(block)
        flat = c_ref[:, :, low:high].reshape(slices * rows, high - low)
        acc = across(flat, low, high, shift)
        acc_ref[:, columns] = acc
        parts = [
            filter_rows(acc[i * rows : (i + 1) * rows])[EDGE : rows - EDGE]
            for i in range(slices)
        ]
        advance(block, columns, parts)

    for there, side, device in ((has_up, 0, up), (has_down, 1, down)):
        @pl.when(there)
        def _(side=side, device=device):
            halo_copy(1 - side, device).wait_recv()

    for block in range(blocks):
        columns = slice(block * BLOCK, (block + 1) * BLOCK)
        low, high, shift = span(block)
        halo = jnp.concatenate([halo_in[0, :, low:high], halo_in[1, :, low:high]], axis=0)
        halo = across(halo.astype(jnp.bfloat16), low, high, shift)
        above, below = halo[0 : 2 * slices], halo[2 * slices :]
        parts = []
        for i in range(slices):
            first, last = i * rows, (i + 1) * rows
            top = jnp.concatenate(
                [pltpu.roll(above, (6 - 2 * i) % 8, 0), acc_ref[first : first + 16, columns]],
                axis=0,
            )
            bottom = jnp.concatenate(
                [acc_ref[last - 16 : last, columns], pltpu.roll(below, (8 - 2 * i) % 8, 0)],
                axis=0,
            )
            parts.append(
                jnp.concatenate([filter_rows(top)[8:16], filter_rows(bottom)[8:16]], axis=0)
            )
        advance(blocks + block, columns, parts)

    @pl.when(has_prev)
    def _():
        dist_copy.wait_recv()
        entered = jnp.concatenate([dist_in[0:1, :]] * (BLOCK // 128), axis=1)
        ratio = [entered * inverse[i] for i in range(slices)]
        for chunk in range(chunks):
            block = chunk % blocks
            columns = slice(block * BLOCK, (block + 1) * BLOCK)
            chain_copy(chunk).wait_recv()
            before = got[chunk, 0].astype(jnp.float32)
            change = got[chunk, 1].astype(jnp.float32) - before
            maps = [
                take(chunk, columns, i) + (before + ratio[i] * change) for i in range(slices)
            ]

            @pl.when(has_next)
            def _():
                sent[chunk, 0] = (before + plain_ref[chunk]).astype(sent.dtype)
                sent[chunk, 1] = maps[-1].astype(sent.dtype)
                chain_copy(chunk).start()

            put(chunk, columns, maps)

    for there, side, device in ((has_up, 0, up), (has_down, 1, down)):
        @pl.when(there)
        def _(side=side, device=device):
            halo_copy(side, device).wait_send()

    @pl.when(has_next)
    def _():
        dist_copy.wait_send()
        for chunk in range(chunks):
            chain_copy(chunk).wait_send()


def local(n_gz, n_row, contrast, lens_weight, distances):
    slices, rows, cols = contrast.shape
    wire = jnp.bfloat16 if n_gz <= 8 else jnp.float32
    chunks = 2 * (cols // BLOCK)
    mid = rows - 2 * EDGE
    assert mid == 2 * EDGE and 2 * slices == EDGE and cols % BLOCK == 0
    return pl.pallas_call(
        functools.partial(kernel, n_gz, n_row),
        out_shape=jax.ShapeDtypeStruct((slices, rows, cols), jnp.float32),
        in_specs=[
            pl.BlockSpec(memory_space=pl.ANY),
            pl.BlockSpec(memory_space=pltpu.SMEM),
            pl.BlockSpec(memory_space=pltpu.SMEM),
        ],
        out_specs=pl.BlockSpec(memory_space=pltpu.VMEM),
        scratch_shapes=[
            pltpu.VMEM((slices, rows, cols), jnp.bfloat16),
            pltpu.VMEM((BLOCK + 2 * REACH, BLOCK), jnp.bfloat16),
            pltpu.VMEM((slices * rows, cols), jnp.float32),
            pltpu.VMEM((2, 2 * slices, cols), jnp.bfloat16),
            pltpu.VMEM((2, 2 * slices, cols), jnp.bfloat16),
            pltpu.VMEM((8, 128), jnp.float32),
            pltpu.VMEM((8, 128), jnp.float32),
            pltpu.VMEM((chunks, mid, BLOCK), jnp.float32),
            pltpu.VMEM((chunks, 2, mid, BLOCK), wire),
            pltpu.VMEM((chunks, 2, mid, BLOCK), wire),
            pltpu.SemaphoreType.DMA,
            pltpu.SemaphoreType.DMA((2,)),
            pltpu.SemaphoreType.DMA((2,)),
            pltpu.SemaphoreType.DMA((2,)),
            pltpu.SemaphoreType.DMA((chunks,)),
            pltpu.SemaphoreType.DMA((chunks,)),
        ],
        compiler_params=pltpu.CompilerParams(
            collective_id=0, has_side_effects=True, vmem_limit_bytes=8 * 1024 * 1024
        ),
    )(contrast, lens_weight, distances)


def solution(mesh):
    return jax.shard_map(
        functools.partial(local, mesh.shape["gz"], mesh.shape["row"]),
        mesh=mesh,
        in_specs=(P(("patch", "gz"), "row", None), P("gz"), P(None, "gz")),
        out_specs=P(("patch", "gz"), "row", None),
        check_vma=False,
    )
```

time: 74.5 us -> 15.2 us (0.20)
  the two profiles are of different devices: /device:TPU:0 before, /device:TPU:29 now
where the time goes in v1:
time: 15.2 us; the launch traced here: 15 us
  Pallas kernels  12 us (79%)
  local copies, waits for them, and re-layouts  3.08 us (20%)
    pallas_call x1, Pallas kernels, local(): pl.pallas_call(functools.partial(kernel, n_gz, n_row), out_shape=jax.Shap...  12 us
    unnamed x7, local copies, waits for them, and re-layouts  3.08 us

profile of v1, /device:TPU:29, one launch (start us, length us, event | category | flops | bytes accessed | tf_op | source)
XLA Modules:
  0.0 15.0 jit_solution(9560914832481992705)
XLA Ops:
  0.0 0.0 copy-start
  0.0 0.9 %copy-done = bf16[4,32,1024]{2,1,0:T(8,128)(2,1)S(1)} copy-done((bf16[4,32,1024]{2,1,0:T(8,128)(2,1)S(1)}, bf16[4,32,1024]{2,1,0:T(8,128)(2,1)}, u32[]{:S(2)}) %copy-start) | copy-done | bytes 262168
  1.0 0.0 copy-start.1
  1.0 0.7 %copy-done.1 = f32[2,4]{1,0:T(2,128)S(1)} copy-done((f32[2,4]{1,0:T(2,128)S(1)}, f32[2,4]{1,0:T(2,128)}, u32[]{:S(2)}) %copy-start.1) | copy-done | bytes 56
  1.6 0.0 copy-start.2
  1.6 0.7 %copy-done.2 = f32[4]{0:T(128)S(1)} copy-done((f32[4]{0:T(128)S(1)}, f32[4]{0:T(128)}, u32[]{:S(2)}) %copy-start.2) | copy-done | bytes 40
  2.3 12.0 %shard_map.37 = f32[4,32,1024]{2,1,0:T(8,128)S(1)} custom-call(bf16[4,32,1024]{2,1,0:T(8,128)(2,1)S(1)} %copy-done, f32[4]{0:T(128)S(1)} %copy-done.2, f32[2,4]{1,0:T(2,128)S(1)} %copy-done.1), custom_call_target="tpu_custom_call" | custom-call | tf_op jit(solution)/shard_map/pallas_call | solution.py:232
  14.2 0.8 %copy.5 = f32[4,32,1024]{2,1,0:T(8,128)} copy(f32[4,32,1024]{2,1,0:T(8,128)S(1)} %shard_map.37) | data formatting | bytes 1048576
Async XLA Ops:
  0.0 0.9 %copy-start = (bf16[4,32,1024]{2,1,0:T(8,128)(2,1)S(1)}, bf16[4,32,1024]{2,1,0:T(8,128)(2,1)}, u32[]{:S(2)}) copy-start(bf16[4,32,1024]{2,1,0:T(8,128)(2,1)} %c_hbm.1) | copy-start | bytes 786436
  1.0 0.7 %copy-start.1 = (f32[2,4]{1,0:T(2,128)S(1)}, f32[2,4]{1,0:T(2,128)}, u32[]{:S(2)}) copy-start(f32[2,4]{1,0:T(2,128)} %dist_ref.1) | copy-start | bytes 100
  1.6 0.7 %copy-start.2 = (f32[4]{0:T(128)S(1)}, f32[4]{0:T(128)}, u32[]{:S(2)}) copy-start(f32[4]{0:T(128)} %weight_ref.1) | copy-start | bytes 52

commit v2 on v1

--- a/solution.py
+++ b/solution.py
@@ -23,9 +23,9 @@
 
 
 def kernel(
-    n_gz, n_row, c_hbm, weight_ref, dist_ref, out_ref,
-    c_ref, beam_ref, acc_ref, halo_out, halo_in, dist_out, dist_in, plain_ref,
-    sent, got, load_sem, halo_send, halo_recv, dist_sems, chain_send, chain_recv,
+    n_gz, n_row, c_hbm, weight_hbm, dist_hbm, out_hbm,
+    out_ref, weight_ref, dist_ref, c_ref, beam_ref, acc_ref, halo_out, halo_in, dist_out, dist_in, plain_ref,
+    sent, got, load_sems, halo_send, halo_recv, dist_sems, chain_send, chain_recv, store_sems,
 ):
     slices, rows, cols = c_ref.shape
     blocks = cols // BLOCK
@@ -37,8 +37,14 @@
     up, down = {"row": row - 1}, {"row": row + 1}
     prev, nxt = {"gz": gz - 1}, {"gz": gz + 1}
 
-    load = pltpu.make_async_copy(c_hbm, c_ref, load_sem)
+    load = pltpu.make_async_copy(c_hbm, c_ref, load_sems.at[0])
     load.start()
+    small = [
+        pltpu.make_async_copy(weight_hbm, weight_ref, load_sems.at[1]),
+        pltpu.make_async_copy(dist_hbm, dist_ref, load_sems.at[2]),
+    ]
+    for copy in small:
+        copy.start()
     barrier = pltpu.get_barrier_semaphore()
     for there, device in ((has_up, up), (has_down, down), (has_prev, prev)):
         @pl.when(there)
@@ -64,12 +70,14 @@
         recv_sem=dist_sems.at[1], device_id=nxt, device_id_type=MESH,
     )
 
-    dist_out[...] = jnp.full(dist_out.shape, dist_ref[1, slices - 1], jnp.float32)
     window = BLOCK + 2 * REACH
     source = lax.broadcasted_iota(jnp.int32, (window, BLOCK), 0)
     target = lax.broadcasted_iota(jnp.int32, (window, BLOCK), 1)
     offset = (source - REACH - target).astype(jnp.float32)
     beam_ref[...] = (jnp.exp(-offset * offset) / math.sqrt(math.pi)).astype(jnp.bfloat16)
+    for copy in small:
+        copy.wait()
+    dist_out[...] = jnp.full(dist_out.shape, dist_ref[1, slices - 1], jnp.float32)
     ones = jnp.ones((1, BLOCK), jnp.float32)
     weight = [ones * weight_ref[i] for i in range(slices)]
     weight_near = [weight[i] * dist_ref[0, i] for i in range(slices)]
@@ -125,14 +133,33 @@
             plain = plain + weight[i] * parts[i]
             dist = dist + weight_near[i] * parts[i]
             maps.append(plain - dist * inverse[i])
-        put(chunk, columns, maps)
-        plain_ref[chunk] = plain
 
         @pl.when(jnp.logical_and(has_next, jnp.logical_not(has_prev)))
         def _():
             sent[chunk, 0] = plain.astype(sent.dtype)
             sent[chunk, 1] = maps[-1].astype(sent.dtype)
             chain_copy(chunk).start()
+
+        put(chunk, columns, maps)
+        plain_ref[chunk] = plain
+
+        @pl.when(jnp.logical_not(has_prev))
+        def _():
+            for copy in stores(chunk):
+                copy.start()
+
+    def stores(chunk):
+        block = chunk % blocks
+        columns = slice(block * BLOCK, (block + 1) * BLOCK)
+        spans = [(EDGE, rows - EDGE)] if chunk < blocks else [(0, EDGE), (rows - EDGE, rows)]
+        return [
+            pltpu.make_async_copy(
+                out_ref.at[:, low:high, columns],
+                out_hbm.at[:, low:high, columns],
+                store_sems.at[chunk, side],
+            )
+            for side, (low, high) in enumerate(spans)
+        ]
 
     def put(chunk, columns, maps):
         for i in range(slices):
@@ -210,6 +237,8 @@
                 chain_copy(chunk).start()
 
             put(chunk, columns, maps)
+            for copy in stores(chunk):
+                copy.start()
 
     for there, side, device in ((has_up, 0, up), (has_down, 1, down)):
         @pl.when(there)
@@ -221,6 +250,10 @@
         dist_copy.wait_send()
         for chunk in range(chunks):
             chain_copy(chunk).wait_send()
+
+    for chunk in range(chunks):
+        for copy in stores(chunk):
+            copy.wait()
 
 
 def local(n_gz, n_row, contrast, lens_weight, distances):
@@ -234,11 +267,14 @@
         out_shape=jax.ShapeDtypeStruct((slices, rows, cols), jnp.float32),
         in_specs=[
             pl.BlockSpec(memory_space=pl.ANY),
-            pl.BlockSpec(memory_space=pltpu.SMEM),
-            pl.BlockSpec(memory_space=pltpu.SMEM),
+            pl.BlockSpec(memory_space=pl.ANY),
+            pl.BlockSpec(memory_space=pl.ANY),
         ],
-        out_specs=pl.BlockSpec(memory_space=pltpu.VMEM),
+        out_specs=pl.BlockSpec(memory_space=pl.ANY),
         scratch_shapes=[
+            pltpu.VMEM((slices, rows, cols), jnp.float32),
+            pltpu.SMEM(lens_weight.shape, jnp.float32),
+            pltpu.SMEM(distances.shape, jnp.float32),
             pltpu.VMEM((slices, rows, cols), jnp.bfloat16),
             pltpu.VMEM((BLOCK + 2 * REACH, BLOCK), jnp.bfloat16),
             pltpu.VMEM((slices * rows, cols), jnp.float32),
@@ -249,15 +285,16 @@
             pltpu.VMEM((chunks, mid, BLOCK), jnp.float32),
             pltpu.VMEM((chunks, 2, mid, BLOCK), wire),
             pltpu.VMEM((chunks, 2, mid, BLOCK), wire),
-            pltpu.SemaphoreType.DMA,
+            pltpu.SemaphoreType.DMA((3,)),
             pltpu.SemaphoreType.DMA((2,)),
             pltpu.SemaphoreType.DMA((2,)),
             pltpu.SemaphoreType.DMA((2,)),
             pltpu.SemaphoreType.DMA((chunks,)),
             pltpu.SemaphoreType.DMA((chunks,)),
+            pltpu.SemaphoreType.DMA((chunks, 2)),
         ],
         compiler_params=pltpu.CompilerParams(
-            collective_id=0, has_side_effects=True, vmem_limit_bytes=8 * 1024 * 1024
+            collective_id=0, has_side_effects=True, vmem_limit_bytes=59_000_000
         ),
     )(contrast, lens_weight, distances)
 

time: 15.2 us -> 14.2 us (0.934)
  local copies, waits for them, and re-layouts: 3.08 us -> 1.89 us
    unnamed x7 -> x1, local copies, waits for them, and re-layouts: 3.08 us -> 1.89 us
    pallas_call x1, Pallas kernels: 12 us -> 12.1 us  [local(): pl.pallas_call(functools.partial(kernel, n_gz, n_row), out_shape=jax.Shap...]
where the time goes in v2:
time: 14.2 us; the launch traced here: 14 us
  Pallas kernels  12.1 us (85%)
  local copies, waits for them, and re-layouts  1.89 us (13%)
    pallas_call x1, Pallas kernels, local(): pl.pallas_call(functools.partial(kernel, n_gz, n_row), out_shape=jax.Shap...  12.1 us
    unnamed x1, local copies, waits for them, and re-layouts  1.89 us

profile of v2, /device:TPU:29, one launch (start us, length us, event | category | flops | bytes accessed | tf_op | source)
XLA Modules:
  0.0 14.0 jit_solution(1328837634416870591)
XLA Ops:
  0.0 12.1 %shard_map.37 = f32[4,32,1024]{2,1,0:T(8,128)} custom-call(bf16[4,32,1024]{2,1,0:T(8,128)(2,1)} %c_hbm.1, f32[4]{0:T(128)} %weight_hbm.1, f32[2,4]{1,0:T(2,128)} %dist_hbm.1), custom_call_target="tpu_custom_call" | custom-call | tf_op jit(solution)/shard_map/pallas_call | solution.py:265
  12.2 1.9 %copy.5 = f32[4,32,1024]{2,1,0:T(8,128)} copy(f32[4,32,1024]{2,1,0:T(8,128)} %shard_map.37) | data formatting | bytes 1048576
